TPU v7x, 8 devices: a whole 2x2x1 slice. The times are simulated.
8 devices in a mesh: seqs: 1 (over z), states: 8 (over y, x, core).
Axes of the slice: x: 2, y: 2, z: 1, core: 2. Of those that a mesh axis runs over, the one named last changes fastest.
Arguments:
- trans_mat: bfloat16 [16384, 16384], P(None, 'states')
- emit_mat: bfloat16 [16384, 10000], P('states')
- init_prob: float32 [16384], P('states')
- tokens: int32 [128, 64], P('seqs')
- lengths: int32 [128], P('seqs')
Outputs:
- output 1: float32 [128], P('seqs')
- output 2: float32 [128, 16384], P('seqs', 'states')
All inputs are finite; a program needn't handle non-finite values.
Results may differ from a plain program's by a relative error of at most 0.001.
Values are sent between devices in bfloat16 or wider.
A program may use at most 1 GiB of HBM per device.

v0:
```python
import functools

import jax
import jax.numpy as jnp
from jax import lax
from jax.experimental import pallas as pl
from jax.experimental.pallas import tpu as pltpu
from jax.sharding import PartitionSpec as P

N_DEV = 8
SEQS = 128
OWN = 2048
PIECE = 512
WIDE = 256
STEPS = 63
SEGMENT = 9
ROWS = (32, 48, 64, 80, 96, 112, 128)
REPEATS = {32: 3, 48: 2, 64: 2}
BF16 = jnp.bfloat16
F32 = jnp.float32


def place(g, k):
    late = g // 6
    mid = (g + 6) // 8 - late
    low = 1 - mid - late
    odd = k % 2
    direct = 1 - k // 2
    r = low * g + mid * (2 + 2 * odd + direct) + late * (7 - direct)
    j = low * k + mid * ((g - 2 + 2 * odd) % 4) + late * (g - 6 + 2 * odd)
    return r, j


def distances(me):
    core = me % 2
    xx = (me // 2) % 2
    yy = me // 4

    def dev(r):
        return me + (r % 2) * (1 - 2 * core) + ((r // 2) % 2) * (2 - 4 * xx) + (r // 4) * (4 - 8 * yy)

    return dev


def remote_copy(dev, src, dst, send, recv, r):
    return pltpu.make_async_remote_copy(
        src_ref=src, dst_ref=dst, send_sem=send, recv_sem=recv,
        device_id={"states": dev(r)}, device_id_type=pl.DeviceIdType.MESH,
    )


def signal_all(dev):
    barrier = pltpu.get_barrier_semaphore()
    for r in range(1, N_DEV):
        pl.semaphore_signal(barrier, inc=1, device_id={"states": dev(r)}, device_id_type=pl.DeviceIdType.MESH)
    return barrier


def send_sums(me, dev, sums, part, send, recv):
    part[me] = jnp.sum(sums[...].T, axis=0, keepdims=True)
    for r in range(N_DEV - 1, 0, -1):
        remote_copy(dev, part.at[me], part.at[me], send, recv, r).start()


def add_sums(part, recv):
    pltpu.make_async_copy(part.at[pl.ds(0, 7)], part.at[pl.ds(0, 7)], recv).wait()
    whole = part[0]
    for d in range(1, N_DEV):
        whole = whole + part[d]
    return whole


def first_kernel(raw, alpha, ll, part, sums, send, recv):
    me = lax.axis_index("states")
    dev = distances(me)
    barrier = signal_all(dev)
    both = jnp.zeros((SEQS, 128), F32)
    for q in range(16):
        both = both + raw[:, q * 128:(q + 1) * 128]
    sums[...] = both
    pl.semaphore_wait(barrier, N_DEV - 1)
    send_sums(me, dev, sums, part, send, recv)
    norm = add_sums(part, recv)
    ll[...] = jnp.log(norm)
    scale = jnp.broadcast_to(1.0 / norm, (128, 128)).T
    for q in range(16):
        alpha[:, q * 128:(q + 1) * 128] = raw[:, q * 128:(q + 1) * 128] * scale
    pltpu.make_async_copy(part.at[pl.ds(0, 7)], part.at[pl.ds(0, 7)], send).wait()


def run_first(number, raw):
    vmem = pl.BlockSpec(memory_space=pltpu.VMEM)
    return pl.pallas_call(
        first_kernel,
        out_shape=(jax.ShapeDtypeStruct((SEQS, OWN), F32), jax.ShapeDtypeStruct((1, SEQS), F32)),
        in_specs=[vmem],
        out_specs=(vmem, vmem),
        scratch_shapes=[
            pltpu.VMEM((N_DEV, 1, 128), F32),
            pltpu.VMEM((128, 128), F32),
            pltpu.SemaphoreType.DMA,
            pltpu.SemaphoreType.DMA,
        ],
        compiler_params=pltpu.CompilerParams(collective_id=number, has_side_effects=True, vmem_limit_bytes=8 << 20),
        name="first",
    )(raw)


def step_kernel(m, steps, depth, t0_ref, a_hbm, e_hbm, st_in, len_row, ll_in, st_out, ll_out,
                fixed, ring, gath, e_buf, st, acc, part, sums, recip, len_col,
                fixed_sem, ring_sem, e_sem, st_sem, recv_sem, own_sem, fwd_sem, c_send, c_recv):
    me = lax.axis_index("states")
    dev = distances(me)

    def remote(src, dst, send, recv, r):
        return remote_copy(dev, src, dst, send, recv, r)

    def rows_of(pos):
        r, j = place(pos // 4, pos % 4)
        return a_hbm.at[pl.ds(pl.multiple_of(dev(r) * OWN + j * PIECE, PIECE), PIECE)]

    def begins(b):
        return 4 * b + 2 * ((b + 6) // 8)

    def ring_copy(b):
        return pltpu.make_async_copy(rows_of(begins(b) + 1), ring.at[b % depth], ring_sem.at[b % depth])

    def start_fixed(b, positions):
        for k, pos in enumerate(positions):
            pltpu.make_async_copy(rows_of(pos), fixed.at[3 * b + k], fixed_sem.at[b]).start()

    def start_block(b):
        start_fixed(b, [begins(b), begins(b) + 2, begins(b) + 3])

    def wait_fixed(b):
        pltpu.make_async_copy(fixed.at[pl.ds(3 * b, 3)], fixed.at[pl.ds(3 * b, 3)], fixed_sem.at[b]).wait()

    def send_piece(slot, j, r, pos):
        remote(gath.at[slot, j], gath.at[slot, pos], own_sem.at[slot], recv_sem.at[slot, pos], r).start()

    def send_pair(slot, j):
        send_piece(slot, j, 3, 8 + 4 * j)
        send_piece(slot, j + 2, 5, 9 + 4 * j)
        send_piece(slot, j, 1, 4 + j)
        send_piece(slot, j + 2, 1, 6 + j)

    def send_rest(slot):
        for j in range(2):
            send_piece(slot, j + 2, 3, 16 + 4 * j)
            send_piece(slot, j, 5, 17 + 4 * j)

    def received(slot, pos):
        pltpu.make_async_copy(gath.at[slot, pos], gath.at[slot, pos], recv_sem.at[slot, pos]).wait()

    def forward(slot, pos, to, r):
        remote(gath.at[slot, pos], gath.at[slot, to], fwd_sem.at[slot], recv_sem.at[slot, to], r).start()

    def arrived(slot, g, relay):
        for k in range(2):
            pos = 4 * g + k
            received(slot, pos)

            @pl.when(relay)
            def _():
                forward(slot, pos, pos + 16, 5 - 2 * k)

            forward(slot, pos, pos + 2, 1)

    def product(parts, n):
        cols = slice(n * WIDE, (n + 1) * WIDE)
        got = None
        for left, right in parts:
            rows = left[...]
            if m in REPEATS:
                rows = jnp.concatenate([rows] * REPEATS[m], axis=0)
            one = jnp.dot(rows, right[:, cols], preferred_element_type=F32)
            got = one if got is None else got + one
        return got[:m]

    def next_ring(b):
        ring_copy((b + depth - 1) % 8).start()

    st_copy = pltpu.make_async_copy(st_in.at[pl.ds(0, m)], st, st_sem.at[0])
    st_copy.start()
    ring_copy(0).start()
    start_block(0)
    for b in range(1, depth - 1):
        ring_copy(b).start()
    start_block(1)
    pltpu.make_async_copy(e_hbm.at[0], e_buf, e_sem.at[0]).start()

    barrier = signal_all(dev)
    if m < SEQS:
        sums[...] = jnp.zeros_like(sums)
    t0 = t0_ref[0]
    lens_row = len_row[...]
    len_col[...] = jnp.broadcast_to(lens_row.astype(F32), (128, 128)).T

    def total(slot):
        send_sums(me, dev, sums, part.at[slot], c_send.at[slot], c_recv.at[slot])

    def total_done(slot):
        norm = add_sums(part.at[slot], c_recv.at[slot])
        recip[...] = jnp.broadcast_to(1.0 / norm, (128, 128)).T
        return norm

    def total_sent(slot):
        pltpu.make_async_copy(part.at[slot, pl.ds(0, 7)], part.at[slot, pl.ds(0, 7)], c_send.at[slot]).wait()

    ll_out[...] = ll_in[...]
    st_copy.wait()
    pl.semaphore_wait(barrier, N_DEV - 1)
    for j in range(2):
        for i in (j, j + 2):
            gath[0, i] = st[:, i * PIECE:(i + 1) * PIECE].astype(BF16)
        send_pair(0, j)
    send_rest(0)

    def one_step(s, carry):
        slot = s % 2
        then = 1 - slot

        def block(b, carry):
            @pl.when(b == 1)
            def _():
                for k in range(4):
                    received(slot, 4 + k)

            @pl.when(b == 2)
            def _():
                arrived(slot, 2, True)

                @pl.when(s == 0)
                def _():
                    wait_fixed(7)
                    start_block(3)

                for n in range(8):
                    acc[n] += product([(gath.at[slot, 8], fixed.at[21]), (gath.at[slot, 9], fixed.at[22])], n)

            @pl.when(b >= 2)
            def _():
                arrived(slot, b + 1, b == 2)
                received(slot, 4 * b + 2)
                received(slot, 4 * b + 3)

            next_ring(b)

            @pl.when(s == 0)
            def _():
                wait_fixed(b)

                @pl.when(b == 0)
                def _():
                    start_fixed(7, [8, 9, 30])

                @pl.when(b == 1)
                def _():
                    start_block(2)

                @pl.when((b - 1) * (5 - b) > 0)
                def _():
                    start_block(b + 2)

            ring_copy(b).wait()
            left = [gath.at[slot, begins(b) + k] for k in range(4)]
            right = [fixed.at[3 * b], ring.at[b % depth], fixed.at[3 * b + 1], fixed.at[3 * b + 2]]
            for n in range(8):
                acc[n] = jnp.where(b > 0, acc[n], 0.0) + product(list(zip(left, right)), n)
            return carry

        lax.fori_loop(0, 7, block, 0)

        received(slot, 30)
        received(slot, 31)
        next_ring(7)
        ring_copy(7).wait()
        parts = [(gath.at[slot, 30], fixed.at[23]), (gath.at[slot, 31], ring.at[7 % depth])]
        pltpu.make_async_copy(e_hbm.at[s], e_buf, e_sem.at[0]).wait()
        both = jnp.zeros((m, 128), F32)
        for n in range(8):
            a = (acc[n] + product(parts, n)) * e_buf[:, n * WIDE:(n + 1) * WIDE].astype(F32)
            acc[n] = a
            both = both + (a[:, :128] + a[:, 128:])
        sums[:m] = both

        total(slot)

        @pl.when(s + 1 < steps)
        def _():
            pltpu.make_async_copy(e_hbm.at[s + 1], e_buf, e_sem.at[0]).start()

        pltpu.make_async_copy(gath.at[slot, pl.ds(0, 12)], gath.at[slot, pl.ds(0, 12)], own_sem.at[slot]).wait()
        pltpu.make_async_copy(gath.at[slot, pl.ds(0, 16)], gath.at[slot, pl.ds(0, 16)], fwd_sem.at[slot]).wait()
        norm = total_done(slot)
        t = t0 + s
        ll_out[...] = ll_out[...] + jnp.where(t < lens_row, jnp.log(norm), 0.0)
        total_sent(slot)

        scale = recip[:m]
        live = t.astype(F32) < len_col[:m]
        for j in range(2):
            for i in (j, j + 2):
                for q in range(4):
                    at = i * PIECE + q * 128
                    cols = slice(at, at + 128)
                    new = jnp.where(live, acc[at // WIDE, :, (q % 2) * 128:(q % 2 + 1) * 128] * scale, st[:, cols])
                    st[:, cols] = new
                    gath[then, i, :, q * 128:(q + 1) * 128] = new.astype(BF16)

            @pl.when(s + 1 < steps)
            def _():
                send_pair(then, j)

        @pl.when(s + 1 < steps)
        def _():
            send_rest(then)

        return carry

    lax.fori_loop(0, steps, one_step, 0)

    for b in range(depth - 1):
        ring_copy(b).wait()
    out_copy = pltpu.make_async_copy(st, st_out.at[pl.ds(0, m)], st_sem.at[0])
    out_copy.start()
    out_copy.wait()


def pick_kernel(size, ahead, rows, mods, emit, out, blocks, sem):
    i = pl.program_id(0)
    slots = ahead + 1

    def start(g):
        for q in range(size):
            row = pl.multiple_of(rows[g * size + q], 8)
            pltpu.make_async_copy(
                emit.at[pl.ds(row, 8)], blocks.at[g % slots, pl.ds(8 * q, 8)], sem.at[g % slots]
            ).start()

    @pl.when(i == 0)
    def _():
        def some(g, carry):
            start(g)
            return carry

        lax.fori_loop(0, ahead, some, 0)

    @pl.when(i + ahead < pl.num_programs(0))
    def _():
        start(i + ahead)

    slot = i % slots
    pltpu.make_async_copy(blocks.at[slot], blocks.at[slot], sem.at[slot]).wait()
    row = lax.broadcasted_iota(jnp.int32, (size, 8 * size), 0)
    col = lax.broadcasted_iota(jnp.int32, (size, 8 * size), 1)
    want = row * 8 + jnp.concatenate([mods[...]] * (8 * size // 128), axis=1)
    ones = (col == want).astype(F32).astype(BF16)
    out[...] = jnp.dot(ones, blocks[slot], preferred_element_type=F32).astype(BF16)


def pick_rows(emit, tokens):
    (count,) = tokens.shape
    size = 48 if count % 48 == 0 else 64
    ahead = min(5, count // size)
    mods = jnp.broadcast_to((tokens % 8)[:, None], (count, 128))
    return pl.pallas_call(
        functools.partial(pick_kernel, size, ahead),
        out_shape=jax.ShapeDtypeStruct((count, OWN), BF16),
        grid_spec=pltpu.PrefetchScalarGridSpec(
            num_scalar_prefetch=1,
            grid=(count // size,),
            in_specs=[pl.BlockSpec((size, 128), lambda i, tok: (i, 0)), pl.BlockSpec(memory_space=pl.ANY)],
            out_specs=pl.BlockSpec((size, OWN), lambda i, tok: (i, 0)),
            scratch_shapes=[pltpu.VMEM((ahead + 1, 8 * size, OWN), BF16), pltpu.SemaphoreType.DMA((ahead + 1,))],
        ),
        compiler_params=pltpu.CompilerParams(vmem_limit_bytes=60 << 20),
        name="pick",
    )(tokens - tokens % 8, mods, emit)


def run_steps(m, steps, number, t0, trans, emis, state, len_row, log_lik):
    vmem = pl.BlockSpec(memory_space=pltpu.VMEM)
    hbm = pl.BlockSpec(memory_space=pl.ANY)
    depth = 2 if m > 80 else 4
    dma = pltpu.SemaphoreType.DMA
    return pl.pallas_call(
        functools.partial(step_kernel, m, steps, depth),
        out_shape=(jax.ShapeDtypeStruct((SEQS, OWN), F32), jax.ShapeDtypeStruct((1, SEQS), F32)),
        in_specs=[pl.BlockSpec(memory_space=pltpu.SMEM), hbm, hbm, hbm, vmem, vmem],
        out_specs=(hbm, vmem),
        scratch_shapes=[
            pltpu.VMEM((24, PIECE, OWN), BF16),
            pltpu.VMEM((depth, PIECE, OWN), BF16),
            pltpu.VMEM((2, 32, m, PIECE), BF16),
            pltpu.VMEM((m, OWN), BF16),
            pltpu.VMEM((m, OWN), F32),
            pltpu.VMEM((8, m, WIDE), F32),
            pltpu.VMEM((2, N_DEV, 1, 128), F32),
            pltpu.VMEM((128, 128), F32),
            pltpu.VMEM((128, 128), F32),
            pltpu.VMEM((128, 128), F32),
            dma((8,)), dma((depth,)), dma((1,)), dma((1,)), dma((2, 32)), dma((2,)), dma((2,)), dma((2,)), dma((2,)),
        ],
        input_output_aliases={3: 0, 5: 1},
        compiler_params=pltpu.CompilerParams(
            collective_id=number, has_side_effects=True, vmem_limit_bytes=67043328
        ),
        name=f"steps_{m}_{number}",
    )(t0, trans, emis, state, len_row, log_lik)


def solution(mesh):
    def local_run(trans_cols, emit_rows, init_part, token_rows, length_rows):
        emit_t = emit_rows.T

        def emissions(tokens):
            return pick_rows(emit_t, tokens.reshape(-1)).reshape(*tokens.shape, OWN)

        key = length_rows * SEQS + (SEQS - 1 - jnp.arange(SEQS, dtype=jnp.int32))
        rank = jnp.sum((key[None, :] > key[:, None]).astype(jnp.int32), axis=1)
        pick = (rank[None, :] == jnp.arange(SEQS, dtype=jnp.int32)[:, None]).astype(jnp.int32)
        lens = jnp.sum(pick * length_rows[None, :], axis=1)
        tokens = jnp.sum(token_rows.T[:, None, :] * pick[None], axis=2)
        len_row = lens[None, :]

        def segment(m, number, t0, state, log_lik):
            part = lax.dynamic_slice_in_dim(tokens, t0, SEGMENT, axis=0)[:, :m]
            return run_steps(m, SEGMENT, number, jnp.reshape(t0, (1,)), trans_cols, emissions(part), state,
                             len_row, log_lik)

        state, log_lik = run_first(0, init_part[None, :] * emissions(tokens[0]).astype(F32))

        segs = jnp.arange(STEPS // SEGMENT, dtype=jnp.int32)
        live = jnp.sum((lens[None, :] > 1 + SEGMENT * segs[:, None]).astype(jnp.int32), axis=1)
        which = sum((live > m).astype(jnp.int32) for m in ROWS[:-1])
        plan = jnp.sum(which << (3 * segs))

        def later(seg, carried):
            branches = [functools.partial(segment, m, 1 + i) for i, m in enumerate(ROWS)]
            return lax.switch((plan >> (3 * seg)) & 7, branches, 1 + SEGMENT * seg, *carried)

        state, log_lik = lax.fori_loop(0, STEPS // SEGMENT, later, (state, log_lik))
        return jnp.take(log_lik[0], rank, mode="clip"), jnp.take(state, rank, axis=0, mode="clip")

    return jax.shard_map(
        local_run,
        mesh=mesh,
        in_specs=(P(None, "states"), P("states", None), P("states"), P("seqs", None), P("seqs")),
        out_specs=(P("seqs"), P("seqs", "states")),
        check_vma=False,
    )
```

profile of v0, /device:TPU:0, one launch (start us, length us, event | category | flops | bytes accessed | tf_op | source)
XLA Modules:
  0.0 1410.1 jit_solution(15611549256267473763)
XLA Ops:
  5.9 5.4 pick.15
  12.5 7.8 first.1
  21.9 1382.3 %while.15 = (s32[]{:T(128)}, f32[128,2048]{1,0:T(8,128)}, f32[1,128]{1,0:T(1,128)}, s32[]{:T(128)}, s32[64,128]{1,0:T(8,128)}, /*index=5*/bf16[10000,2048]{1,0:T...) while((s32[]{:T(128)}, f32[128,2048]{1,0:T(8,128)}, ...), condition=%wide.region_13.14_spmd, body=%wide.region_5.13_spmd.sunk | while | flops 13835 | bytes 608567 | solution.py:443
  22.6 243.4 %conditional.2 = ((f32[128,2048]{1,0:T(8,128)}, f32[1,128]{1,0:T(1,128)})) conditional(s32[]{:T(128)} %clamp.11, (s32[]{:T(128)}, s32[64,128]{1,0:T(8,128)}, bf16[10000,2048]{1,0:T(8,128)(2,1)}, bf16[16384,2048]{1,0:T(8,128)(2,1)}, f32[128,2048]{1,0:T(8,128)}, /*index=5*/s32[1,128]{1,0:T(1,128)}, ...), branch_computations={%region_6.6_spmd, %region_7.7_spmd, %region_8.8_spmd, %region_9.9_... | conditional | flops 13827 | bytes 608302 | solution.py:441
  25.0 22.1 %pick.14 = bf16[1152,2048]{1,0:T(8,128)(2,1)} custom-call(s32[1152]{0:T(1024)} %get-tuple-element.332.rows, s32[1152,128]{1,0:T(8,128)} %broadcast_in_dim.16.mods, bf16[10000,2048]{1,0:T(8,128)(2,1)} %get-tuple-element.276.emit), custom_call_target="tpu_custom_call" | custom-call | tf_op jit(solution)/shard_map/while/body/eval_jaxpr/cond/branch_6_fun/pick/pallas_call | solution.py:367
  47.1 218.9 %steps_128_7.1 = (f32[128,2048]{1,0:T(8,128)}, f32[1,128]{1,0:T(1,128)}) custom-call(s32[1]{0:T(128)} %bitcast.12.t0_ref, bf16[16384,2048]{1,0:T(8,128)(2,1)} %get-tuple-element.274.a_hbm, bf16[9,128,2048]{2,1,0:T(8,128)(2,1)} %bitcast.35, f32[128,2048]{1,0:T(8,128)} %get-tuple-element.277.st_in, ...), custom_call_target="tpu_custom_call", output_to_operand_aliasing={{0}: (3, {}), {1}: (5, {})} | custom-call | tf_op jit(solution)/shard_map/while/body/eval_jaxpr/cond/branch_6_fun/steps_128_7/pallas_call | solution.py:387
  266.7 224.5 %conditional.2 = ((f32[128,2048]{1,0:T(8,128)}, f32[1,128]{1,0:T(1,128)})) conditional(s32[]{:T(128)} %clamp.11, (s32[]{:T(128)}, s32[64,128]{1,0:T(8,128)}, bf16[10000,2048]{1,0:T(8,128)(2,1)}, bf16[16384,2048]{1,0:T(8,128)(2,1)}, f32[128,2048]{1,0:T(8,128)}, /*index=5*/s32[1,128]{1,0:T(1,128)}, ...), branch_computations={%region_6.6_spmd, %region_7.7_spmd, %region_8.8_spmd, %region_9.9_... | conditional | flops 13827 | bytes 608302 | solution.py:441
  269.2 19.7 %pick.13 = bf16[1008,2048]{1,0:T(8,128)(2,1)} custom-call(s32[1008]{0:T(1024)} %get-tuple-element.330.rows, s32[1008,128]{1,0:T(8,128)} %broadcast_in_dim.14.mods, bf16[10000,2048]{1,0:T(8,128)(2,1)} %get-tuple-element.269.emit), custom_call_target="tpu_custom_call" | custom-call | tf_op jit(solution)/shard_map/while/body/eval_jaxpr/cond/branch_5_fun/pick/pallas_call | solution.py:367
  288.9 202.3 %steps_112_6.1 = (f32[128,2048]{1,0:T(8,128)}, f32[1,128]{1,0:T(1,128)}) custom-call(s32[1]{0:T(128)} %bitcast.10.t0_ref, bf16[16384,2048]{1,0:T(8,128)(2,1)} %get-tuple-element.267.a_hbm, bf16[9,112,2048]{2,1,0:T(8,128)(2,1)} %bitcast.36, f32[128,2048]{1,0:T(8,128)} %get-tuple-element.270.st_in, ...), custom_call_target="tpu_custom_call", output_to_operand_aliasing={{0}: (3, {}), {1}: (5, {})} | custom-call | tf_op jit(solution)/shard_map/while/body/eval_jaxpr/cond/branch_5_fun/steps_112_6/pallas_call | solution.py:387
  491.9 207.5 %conditional.2 = ((f32[128,2048]{1,0:T(8,128)}, f32[1,128]{1,0:T(1,128)})) conditional(s32[]{:T(128)} %clamp.11, (s32[]{:T(128)}, s32[64,128]{1,0:T(8,128)}, bf16[10000,2048]{1,0:T(8,128)(2,1)}, bf16[16384,2048]{1,0:T(8,128)(2,1)}, f32[128,2048]{1,0:T(8,128)}, /*index=5*/s32[1,128]{1,0:T(1,128)}, ...), branch_computations={%region_6.6_spmd, %region_7.7_spmd, %region_8.8_spmd, %region_9.9_... | conditional | flops 13827 | bytes 608302 | solution.py:441
  494.3 17.7 %pick.12 = bf16[864,2048]{1,0:T(8,128)(2,1)} custom-call(s32[864]{0:T(1024)} %get-tuple-element.328.rows, s32[864,128]{1,0:T(8,128)} %broadcast_in_dim.12.mods, bf16[10000,2048]{1,0:T(8,128)(2,1)} %get-tuple-element.262.emit), custom_call_target="tpu_custom_call" | custom-call | tf_op jit(solution)/shard_map/while/body/eval_jaxpr/cond/branch_4_fun/pick/pallas_call | solution.py:367
  512.0 187.3 %steps_96_5.1 = (f32[128,2048]{1,0:T(8,128)}, f32[1,128]{1,0:T(1,128)}) custom-call(s32[1]{0:T(128)} %bitcast.8.t0_ref, bf16[16384,2048]{1,0:T(8,128)(2,1)} %get-tuple-element.260.a_hbm, bf16[9,96,2048]{2,1,0:T(8,128)(2,1)} %bitcast.37, f32[128,2048]{1,0:T(8,128)} %get-tuple-element.263.st_in, ...), custom_call_target="tpu_custom_call", output_to_operand_aliasing={{0}: (3, {}), {1}: (5, {})} | custom-call | tf_op jit(solution)/shard_map/while/body/eval_jaxpr/cond/branch_4_fun/steps_96_5/pallas_call | solution.py:387
  700.1 192.5 %conditional.2 = ((f32[128,2048]{1,0:T(8,128)}, f32[1,128]{1,0:T(1,128)})) conditional(s32[]{:T(128)} %clamp.11, (s32[]{:T(128)}, s32[64,128]{1,0:T(8,128)}, bf16[10000,2048]{1,0:T(8,128)(2,1)}, bf16[16384,2048]{1,0:T(8,128)(2,1)}, f32[128,2048]{1,0:T(8,128)}, /*index=5*/s32[1,128]{1,0:T(1,128)}, ...), branch_computations={%region_6.6_spmd, %region_7.7_spmd, %region_8.8_spmd, %region_9.9_... | conditional | flops 13827 | bytes 608302 | solution.py:441
  702.4 15.6 %pick.11 = bf16[720,2048]{1,0:T(8,128)(2,1)} custom-call(s32[720]{0:T(1024)} %get-tuple-element.326.rows, s32[720,128]{1,0:T(8,128)} %broadcast_in_dim.10.mods, bf16[10000,2048]{1,0:T(8,128)(2,1)} %get-tuple-element.255.emit), custom_call_target="tpu_custom_call" | custom-call | tf_op jit(solution)/shard_map/while/body/eval_jaxpr/cond/branch_3_fun/pick/pallas_call | solution.py:367
  718.1 174.5 %steps_80_4.1 = (f32[128,2048]{1,0:T(8,128)}, f32[1,128]{1,0:T(1,128)}) custom-call(s32[1]{0:T(128)} %bitcast.6.t0_ref, bf16[16384,2048]{1,0:T(8,128)(2,1)} %get-tuple-element.253.a_hbm, bf16[9,80,2048]{2,1,0:T(8,128)(2,1)} %bitcast.38, f32[128,2048]{1,0:T(8,128)} %get-tuple-element.256.st_in, ...), custom_call_target="tpu_custom_call", output_to_operand_aliasing={{0}: (3, {}), {1}: (5, {})} | custom-call | tf_op jit(solution)/shard_map/while/body/eval_jaxpr/cond/branch_3_fun/steps_80_4/pallas_call | solution.py:387
  893.3 170.6 %conditional.2 = ((f32[128,2048]{1,0:T(8,128)}, f32[1,128]{1,0:T(1,128)})) conditional(s32[]{:T(128)} %clamp.11, (s32[]{:T(128)}, s32[64,128]{1,0:T(8,128)}, bf16[10000,2048]{1,0:T(8,128)(2,1)}, bf16[16384,2048]{1,0:T(8,128)(2,1)}, f32[128,2048]{1,0:T(8,128)}, /*index=5*/s32[1,128]{1,0:T(1,128)}, ...), branch_computations={%region_6.6_spmd, %region_7.7_spmd, %region_8.8_spmd, %region_9.9_... | conditional | flops 13827 | bytes 608302 | solution.py:441
  895.6 13.3 pick.10
  908.9 155.0 %steps_64_3.1 = (f32[128,2048]{1,0:T(8,128)}, f32[1,128]{1,0:T(1,128)}) custom-call(s32[1]{0:T(128)} %bitcast.4.t0_ref, bf16[16384,2048]{1,0:T(8,128)(2,1)} %get-tuple-element.246.a_hbm, bf16[9,64,2048]{2,1,0:T(8,128)(2,1)} %bitcast.39, f32[128,2048]{1,0:T(8,128)} %get-tuple-element.249.st_in, ...), custom_call_target="tpu_custom_call", output_to_operand_aliasing={{0}: (3, {}), {1}: (5, {})} | custom-call | tf_op jit(solution)/shard_map/while/body/eval_jaxpr/cond/branch_2_fun/steps_64_3/pallas_call | solution.py:387
  1064.6 172.0 %conditional.2 = ((f32[128,2048]{1,0:T(8,128)}, f32[1,128]{1,0:T(1,128)})) conditional(s32[]{:T(128)} %clamp.11, (s32[]{:T(128)}, s32[64,128]{1,0:T(8,128)}, bf16[10000,2048]{1,0:T(8,128)(2,1)}, bf16[16384,2048]{1,0:T(8,128)(2,1)}, f32[128,2048]{1,0:T(8,128)}, /*index=5*/s32[1,128]{1,0:T(1,128)}, ...), branch_computations={%region_6.6_spmd, %region_7.7_spmd, %region_8.8_spmd, %region_9.9_... | conditional | flops 13827 | bytes 608302 | solution.py:441
  1066.8 10.9 pick.9
  1077.8 158.8 %steps_48_2.1 = (f32[128,2048]{1,0:T(8,128)}, f32[1,128]{1,0:T(1,128)}) custom-call(s32[1]{0:T(128)} %bitcast.2.t0_ref, bf16[16384,2048]{1,0:T(8,128)(2,1)} %get-tuple-element.239.a_hbm, bf16[9,48,2048]{2,1,0:T(8,128)(2,1)} %bitcast.40, f32[128,2048]{1,0:T(8,128)} %get-tuple-element.242.st_in, ...), custom_call_target="tpu_custom_call", output_to_operand_aliasing={{0}: (3, {}), {1}: (5, {})} | custom-call | tf_op jit(solution)/shard_map/while/body/eval_jaxpr/cond/branch_1_fun/steps_48_2/pallas_call | solution.py:387
  1237.3 166.9 %conditional.2 = ((f32[128,2048]{1,0:T(8,128)}, f32[1,128]{1,0:T(1,128)})) conditional(s32[]{:T(128)} %clamp.11, (s32[]{:T(128)}, s32[64,128]{1,0:T(8,128)}, bf16[10000,2048]{1,0:T(8,128)(2,1)}, bf16[16384,2048]{1,0:T(8,128)(2,1)}, f32[128,2048]{1,0:T(8,128)}, /*index=5*/s32[1,128]{1,0:T(1,128)}, ...), branch_computations={%region_6.6_spmd, %region_7.7_spmd, %region_8.8_spmd, %region_9.9_... | conditional | flops 13827 | bytes 608302 | solution.py:441
  1239.5 9.2 pick.8
  1248.6 155.5 %steps_32_1.1 = (f32[128,2048]{1,0:T(8,128)}, f32[1,128]{1,0:T(1,128)}) custom-call(s32[1]{0:T(128)} %bitcast.t0_ref, bf16[16384,2048]{1,0:T(8,128)(2,1)} %get-tuple-element.232.a_hbm, bf16[9,32,2048]{2,1,0:T(8,128)(2,1)} %bitcast.41, f32[128,2048]{1,0:T(8,128)} %get-tuple-element.235.st_in, ...), custom_call_target="tpu_custom_call", output_to_operand_aliasing={{0}: (3, {}), {1}: (5, {})} | custom-call | tf_op jit(solution)/shard_map/while/body/eval_jaxpr/cond/branch_0_fun/steps_32_1/pallas_call | solution.py:387
  (50 shorter events, 29.8 us)
Async XLA Ops:
  1.5 18.9 %copy-start.3 = (s32[128]{0:T(128)}, s32[128]{0:T(128)S(1)}, u32[]{:S(2)}) copy-start(s32[128]{0:T(128)S(1)} %convert_reduce_fusion) | copy-start | bytes 1540
  5.9 5.5 copy-start.2
  5.9 14.4 %copy-start.4 = (s32[128]{0:T(128)S(1)}, s32[128]{0:T(128)}, u32[]{:S(2)}) copy-start(s32[128]{0:T(128)} %param.18) | copy-start | bytes 1540
  20.5 0.5 copy-start.1
  1404.8 3.6 copy-start
where the time goes:
time: 1420 us; the launch traced here: 1410 us
  Pallas kernels  1370 us (96%)
  local copies, waits for them, and re-layouts  17.6 us (1%)
    pallas_call x7, Pallas kernels, run_steps(): pl.pallas_call(functools.partial(step_kernel, m, steps, depth), out_shape...  1250 us
    pallas_call x8, Pallas kernels, pick_rows(): pl.pallas_call(functools.partial(pick_kernel, size, ahead), out_shape=jax...  114 us

commit v1 on v0

--- a/solution.py
+++ b/solution.py
@@ -15,7 +15,6 @@
 STEPS = 63
 SEGMENT = 9
 ROWS = (32, 48, 64, 80, 96, 112, 128)
-REPEATS = {32: 3, 48: 2, 64: 2}
 BF16 = jnp.bfloat16
 F32 = jnp.float32
 
@@ -171,8 +170,8 @@
         got = None
         for left, right in parts:
             rows = left[...]
-            if m in REPEATS:
-                rows = jnp.concatenate([rows] * REPEATS[m], axis=0)
+            if m < SEQS:
+                rows = jnp.concatenate([rows] * (SEQS // m) + [rows[:SEQS % m]] * (SEQS % m > 0), axis=0)
             one = jnp.dot(rows, right[:, cols], preferred_element_type=F32)
             got = one if got is None else got + one
         return got[:m]
@@ -333,9 +332,9 @@
 
     def start(g):
         for q in range(size):
-            row = pl.multiple_of(rows[g * size + q], 8)
+            row = pl.multiple_of(rows[g * size + q], 2)
             pltpu.make_async_copy(
-                emit.at[pl.ds(row, 8)], blocks.at[g % slots, pl.ds(8 * q, 8)], sem.at[g % slots]
+                emit.at[pl.ds(row, 2)], blocks.at[g % slots, pl.ds(2 * q, 2)], sem.at[g % slots]
             ).start()
 
     @pl.when(i == 0)
@@ -352,9 +351,9 @@
 
     slot = i % slots
     pltpu.make_async_copy(blocks.at[slot], blocks.at[slot], sem.at[slot]).wait()
-    row = lax.broadcasted_iota(jnp.int32, (size, 8 * size), 0)
-    col = lax.broadcasted_iota(jnp.int32, (size, 8 * size), 1)
-    want = row * 8 + jnp.concatenate([mods[...]] * (8 * size // 128), axis=1)
+    row = lax.broadcasted_iota(jnp.int32, (size, 2 * size), 0)
+    col = lax.broadcasted_iota(jnp.int32, (size, 2 * size), 1)
+    want = row * 2 + mods[:, :2 * size]
     ones = (col == want).astype(F32).astype(BF16)
     out[...] = jnp.dot(ones, blocks[slot], preferred_element_type=F32).astype(BF16)
 
@@ -362,8 +361,8 @@
 def pick_rows(emit, tokens):
     (count,) = tokens.shape
     size = 48 if count % 48 == 0 else 64
-    ahead = min(5, count // size)
-    mods = jnp.broadcast_to((tokens % 8)[:, None], (count, 128))
+    ahead = min(3, count // size)
+    mods = jnp.broadcast_to((tokens % 2)[:, None], (count, 128))
     return pl.pallas_call(
         functools.partial(pick_kernel, size, ahead),
         out_shape=jax.ShapeDtypeStruct((count, OWN), BF16),
@@ -372,11 +371,11 @@
             grid=(count // size,),
             in_specs=[pl.BlockSpec((size, 128), lambda i, tok: (i, 0)), pl.BlockSpec(memory_space=pl.ANY)],
             out_specs=pl.BlockSpec((size, OWN), lambda i, tok: (i, 0)),
-            scratch_shapes=[pltpu.VMEM((ahead + 1, 8 * size, OWN), BF16), pltpu.SemaphoreType.DMA((ahead + 1,))],
+            scratch_shapes=[pltpu.VMEM((ahead + 1, 2 * size, OWN), BF16), pltpu.SemaphoreType.DMA((ahead + 1,))],
         ),
         compiler_params=pltpu.CompilerParams(vmem_limit_bytes=60 << 20),
         name="pick",
-    )(tokens - tokens % 8, mods, emit)
+    )(tokens - tokens % 2, mods, emit)
 
 
 def run_steps(m, steps, number, t0, trans, emis, state, len_row, log_lik):

time: 1420 us -> 1370 us (0.965)
  Pallas kernels: 1370 us -> 1320 us
    pallas_call x8, Pallas kernels: 114 us -> 84.9 us  [pick_rows(): pl.pallas_call(functools.partial(pick_kernel, size, ahead), out_shape=jax...]
    pallas_call x7, Pallas kernels: 1250 us -> 1230 us  [run_steps(): pl.pallas_call(functools.partial(step_kernel, m, steps, depth), out_shape...]
where the time goes in v1:
time: 1370 us; the launch traced here: 1360 us
  Pallas kernels  1320 us (96%)
  local copies, waits for them, and re-layouts  17.6 us (1%)
    pallas_call x7, Pallas kernels, run_steps(): pl.pallas_call(functools.partial(step_kernel, m, steps, depth), out_shape...  1230 us
    pallas_call x8, Pallas kernels, pick_rows(): pl.pallas_call(functools.partial(pick_kernel, size, ahead), out_shape=jax...  84.9 us

profile of v1, /device:TPU:0, one launch (start us, length us, event | category | flops | bytes accessed | tf_op | source)
XLA Modules:
  0.0 1358.0 jit_solution(4623815370456604417)
XLA Ops:
  5.9 3.9 pick.15
  10.9 7.8 first.1
  20.3 1331.8 %while.15 = (s32[]{:T(128)}, f32[128,2048]{1,0:T(8,128)}, f32[1,128]{1,0:T(1,128)}, s32[]{:T(128)}, s32[64,128]{1,0:T(8,128)}, /*index=5*/bf16[10000,2048]{1,0:T...) while((s32[]{:T(128)}, f32[128,2048]{1,0:T(8,128)}, ...), condition=%wide.region_13.14_spmd, body=%wide.region_5.13_spmd.sunk | while | flops 13835 | bytes 608567 | solution.py:442
  21.0 238.3 %conditional.2 = ((f32[128,2048]{1,0:T(8,128)}, f32[1,128]{1,0:T(1,128)})) conditional(s32[]{:T(128)} %clamp.11, (s32[]{:T(128)}, s32[64,128]{1,0:T(8,128)}, bf16[10000,2048]{1,0:T(8,128)(2,1)}, bf16[16384,2048]{1,0:T(8,128)(2,1)}, f32[128,2048]{1,0:T(8,128)}, /*index=5*/s32[1,128]{1,0:T(1,128)}, ...), branch_computations={%region_6.6_spmd, %region_7.7_spmd, %region_8.8_spmd, %region_9.9_... | conditional | flops 13827 | bytes 608302 | solution.py:440
  23.4 17.0 %pick.14 = bf16[1152,2048]{1,0:T(8,128)(2,1)} custom-call(s32[1152]{0:T(1024)} %get-tuple-element.332.rows, s32[1152,128]{1,0:T(8,128)} %broadcast_in_dim.16.mods, bf16[10000,2048]{1,0:T(8,128)(2,1)} %get-tuple-element.276.emit), custom_call_target="tpu_custom_call" | custom-call | tf_op jit(solution)/shard_map/while/body/eval_jaxpr/cond/branch_6_fun/pick/pallas_call | solution.py:366
  40.4 218.9 %steps_128_7.1 = (f32[128,2048]{1,0:T(8,128)}, f32[1,128]{1,0:T(1,128)}) custom-call(s32[1]{0:T(128)} %bitcast.12.t0_ref, bf16[16384,2048]{1,0:T(8,128)(2,1)} %get-tuple-element.274.a_hbm, bf16[9,128,2048]{2,1,0:T(8,128)(2,1)} %bitcast.35, f32[128,2048]{1,0:T(8,128)} %get-tuple-element.277.st_in, ...), custom_call_target="tpu_custom_call", output_to_operand_aliasing={{0}: (3, {}), {1}: (5, {})} | custom-call | tf_op jit(solution)/shard_map/while/body/eval_jaxpr/cond/branch_6_fun/steps_128_7/pallas_call | solution.py:386
  260.0 219.5 %conditional.2 = ((f32[128,2048]{1,0:T(8,128)}, f32[1,128]{1,0:T(1,128)})) conditional(s32[]{:T(128)} %clamp.11, (s32[]{:T(128)}, s32[64,128]{1,0:T(8,128)}, bf16[10000,2048]{1,0:T(8,128)(2,1)}, bf16[16384,2048]{1,0:T(8,128)(2,1)}, f32[128,2048]{1,0:T(8,128)}, /*index=5*/s32[1,128]{1,0:T(1,128)}, ...), branch_computations={%region_6.6_spmd, %region_7.7_spmd, %region_8.8_spmd, %region_9.9_... | conditional | flops 13827 | bytes 608302 | solution.py:440
  262.5 15.2 %pick.13 = bf16[1008,2048]{1,0:T(8,128)(2,1)} custom-call(s32[1008]{0:T(1024)} %get-tuple-element.330.rows, s32[1008,128]{1,0:T(8,128)} %broadcast_in_dim.14.mods, bf16[10000,2048]{1,0:T(8,128)(2,1)} %get-tuple-element.269.emit), custom_call_target="tpu_custom_call" | custom-call | tf_op jit(solution)/shard_map/while/body/eval_jaxpr/cond/branch_5_fun/pick/pallas_call | solution.py:366
  277.7 201.8 %steps_112_6.1 = (f32[128,2048]{1,0:T(8,128)}, f32[1,128]{1,0:T(1,128)}) custom-call(s32[1]{0:T(128)} %bitcast.10.t0_ref, bf16[16384,2048]{1,0:T(8,128)(2,1)} %get-tuple-element.267.a_hbm, bf16[9,112,2048]{2,1,0:T(8,128)(2,1)} %bitcast.36, f32[128,2048]{1,0:T(8,128)} %get-tuple-element.270.st_in, ...), custom_call_target="tpu_custom_call", output_to_operand_aliasing={{0}: (3, {}), {1}: (5, {})} | custom-call | tf_op jit(solution)/shard_map/while/body/eval_jaxpr/cond/branch_5_fun/steps_112_6/pallas_call | solution.py:386
  480.2 202.2 %conditional.2 = ((f32[128,2048]{1,0:T(8,128)}, f32[1,128]{1,0:T(1,128)})) conditional(s32[]{:T(128)} %clamp.11, (s32[]{:T(128)}, s32[64,128]{1,0:T(8,128)}, bf16[10000,2048]{1,0:T(8,128)(2,1)}, bf16[16384,2048]{1,0:T(8,128)(2,1)}, f32[128,2048]{1,0:T(8,128)}, /*index=5*/s32[1,128]{1,0:T(1,128)}, ...), branch_computations={%region_6.6_spmd, %region_7.7_spmd, %region_8.8_spmd, %region_9.9_... | conditional | flops 13827 | bytes 608302 | solution.py:440
  482.6 13.4 pick.12
  496.0 186.4 %steps_96_5.1 = (f32[128,2048]{1,0:T(8,128)}, f32[1,128]{1,0:T(1,128)}) custom-call(s32[1]{0:T(128)} %bitcast.8.t0_ref, bf16[16384,2048]{1,0:T(8,128)(2,1)} %get-tuple-element.260.a_hbm, bf16[9,96,2048]{2,1,0:T(8,128)(2,1)} %bitcast.37, f32[128,2048]{1,0:T(8,128)} %get-tuple-element.263.st_in, ...), custom_call_target="tpu_custom_call", output_to_operand_aliasing={{0}: (3, {}), {1}: (5, {})} | custom-call | tf_op jit(solution)/shard_map/while/body/eval_jaxpr/cond/branch_4_fun/steps_96_5/pallas_call | solution.py:386
  683.2 183.7 %conditional.2 = ((f32[128,2048]{1,0:T(8,128)}, f32[1,128]{1,0:T(1,128)})) conditional(s32[]{:T(128)} %clamp.11, (s32[]{:T(128)}, s32[64,128]{1,0:T(8,128)}, bf16[10000,2048]{1,0:T(8,128)(2,1)}, bf16[16384,2048]{1,0:T(8,128)(2,1)}, f32[128,2048]{1,0:T(8,128)}, /*index=5*/s32[1,128]{1,0:T(1,128)}, ...), branch_computations={%region_6.6_spmd, %region_7.7_spmd, %region_8.8_spmd, %region_9.9_... | conditional | flops 13827 | bytes 608302 | solution.py:440
  685.5 11.6 pick.11
  697.1 169.8 %steps_80_4.1 = (f32[128,2048]{1,0:T(8,128)}, f32[1,128]{1,0:T(1,128)}) custom-call(s32[1]{0:T(128)} %bitcast.6.t0_ref, bf16[16384,2048]{1,0:T(8,128)(2,1)} %get-tuple-element.253.a_hbm, bf16[9,80,2048]{2,1,0:T(8,128)(2,1)} %bitcast.38, f32[128,2048]{1,0:T(8,128)} %get-tuple-element.256.st_in, ...), custom_call_target="tpu_custom_call", output_to_operand_aliasing={{0}: (3, {}), {1}: (5, {})} | custom-call | tf_op jit(solution)/shard_map/while/body/eval_jaxpr/cond/branch_3_fun/steps_80_4/pallas_call | solution.py:386
  867.6 167.0 %conditional.2 = ((f32[128,2048]{1,0:T(8,128)}, f32[1,128]{1,0:T(1,128)})) conditional(s32[]{:T(128)} %clamp.11, (s32[]{:T(128)}, s32[64,128]{1,0:T(8,128)}, bf16[10000,2048]{1,0:T(8,128)(2,1)}, bf16[16384,2048]{1,0:T(8,128)(2,1)}, f32[128,2048]{1,0:T(8,128)}, /*index=5*/s32[1,128]{1,0:T(1,128)}, ...), branch_computations={%region_6.6_spmd, %region_7.7_spmd, %region_8.8_spmd, %region_9.9_... | conditional | flops 13827 | bytes 608302 | solution.py:440
  869.9 9.7 pick.10
  879.7 155.0 %steps_64_3.1 = (f32[128,2048]{1,0:T(8,128)}, f32[1,128]{1,0:T(1,128)}) custom-call(s32[1]{0:T(128)} %bitcast.4.t0_ref, bf16[16384,2048]{1,0:T(8,128)(2,1)} %get-tuple-element.246.a_hbm, bf16[9,64,2048]{2,1,0:T(8,128)(2,1)} %bitcast.39, f32[128,2048]{1,0:T(8,128)} %get-tuple-element.249.st_in, ...), custom_call_target="tpu_custom_call", output_to_operand_aliasing={{0}: (3, {}), {1}: (5, {})} | custom-call | tf_op jit(solution)/shard_map/while/body/eval_jaxpr/cond/branch_2_fun/steps_64_3/pallas_call | solution.py:386
  1035.4 160.7 %conditional.2 = ((f32[128,2048]{1,0:T(8,128)}, f32[1,128]{1,0:T(1,128)})) conditional(s32[]{:T(128)} %clamp.11, (s32[]{:T(128)}, s32[64,128]{1,0:T(8,128)}, bf16[10000,2048]{1,0:T(8,128)(2,1)}, bf16[16384,2048]{1,0:T(8,128)(2,1)}, f32[128,2048]{1,0:T(8,128)}, /*index=5*/s32[1,128]{1,0:T(1,128)}, ...), branch_computations={%region_6.6_spmd, %region_7.7_spmd, %region_8.8_spmd, %region_9.9_... | conditional | flops 13827 | bytes 608302 | solution.py:440
  1037.6 7.9 pick.9
  1045.6 150.5 %steps_48_2.1 = (f32[128,2048]{1,0:T(8,128)}, f32[1,128]{1,0:T(1,128)}) custom-call(s32[1]{0:T(128)} %bitcast.2.t0_ref, bf16[16384,2048]{1,0:T(8,128)(2,1)} %get-tuple-element.239.a_hbm, bf16[9,48,2048]{2,1,0:T(8,128)(2,1)} %bitcast.40, f32[128,2048]{1,0:T(8,128)} %get-tuple-element.242.st_in, ...), custom_call_target="tpu_custom_call", output_to_operand_aliasing={{0}: (3, {}), {1}: (5, {})} | custom-call | tf_op jit(solution)/shard_map/while/body/eval_jaxpr/cond/branch_1_fun/steps_48_2/pallas_call | solution.py:386
  1196.8 155.3 %conditional.2 = ((f32[128,2048]{1,0:T(8,128)}, f32[1,128]{1,0:T(1,128)})) conditional(s32[]{:T(128)} %clamp.11, (s32[]{:T(128)}, s32[64,128]{1,0:T(8,128)}, bf16[10000,2048]{1,0:T(8,128)(2,1)}, bf16[16384,2048]{1,0:T(8,128)(2,1)}, f32[128,2048]{1,0:T(8,128)}, /*index=5*/s32[1,128]{1,0:T(1,128)}, ...), branch_computations={%region_6.6_spmd, %region_7.7_spmd, %region_8.8_spmd, %region_9.9_... | conditional | flops 13827 | bytes 608302 | solution.py:440
  1199.0 6.2 pick.8
  1205.2 146.9 %steps_32_1.1 = (f32[128,2048]{1,0:T(8,128)}, f32[1,128]{1,0:T(1,128)}) custom-call(s32[1]{0:T(128)} %bitcast.t0_ref, bf16[16384,2048]{1,0:T(8,128)(2,1)} %get-tuple-element.232.a_hbm, bf16[9,32,2048]{2,1,0:T(8,128)(2,1)} %bitcast.41, f32[128,2048]{1,0:T(8,128)} %get-tuple-element.235.st_in, ...), custom_call_target="tpu_custom_call", output_to_operand_aliasing={{0}: (3, {}), {1}: (5, {})} | custom-call | tf_op jit(solution)/shard_map/while/body/eval_jaxpr/cond/branch_0_fun/steps_32_1/pallas_call | solution.py:386
  (50 shorter events, 29.8 us)
Async XLA Ops:
  1.5 17.3 %copy-start.3 = (s32[128]{0:T(128)}, s32[128]{0:T(128)S(1)}, u32[]{:S(2)}) copy-start(s32[128]{0:T(128)S(1)} %convert_reduce_fusion) | copy-start | bytes 1540
  5.9 3.9 copy-start.2
  5.9 12.9 copy-start.4
  18.9 0.5 copy-start.1
  1352.7 3.6 copy-start

commit v2 on v1

--- a/solution.py
+++ b/solution.py
@@ -12,9 +12,10 @@
 OWN = 2048
 PIECE = 512
 WIDE = 256
-STEPS = 63
-SEGMENT = 9
-ROWS = (32, 48, 64, 80, 96, 112, 128)
+SHORT = 9
+SEGMENTS = 7
+ROWS = (64, 80, 96, 112, 128)
+LONG, LONG_ROWS = 3, 64
 BF16 = jnp.bfloat16
 F32 = jnp.float32
 
@@ -69,43 +70,7 @@
     return whole
 
 
-def first_kernel(raw, alpha, ll, part, sums, send, recv):
-    me = lax.axis_index("states")
-    dev = distances(me)
-    barrier = signal_all(dev)
-    both = jnp.zeros((SEQS, 128), F32)
-    for q in range(16):
-        both = both + raw[:, q * 128:(q + 1) * 128]
-    sums[...] = both
-    pl.semaphore_wait(barrier, N_DEV - 1)
-    send_sums(me, dev, sums, part, send, recv)
-    norm = add_sums(part, recv)
-    ll[...] = jnp.log(norm)
-    scale = jnp.broadcast_to(1.0 / norm, (128, 128)).T
-    for q in range(16):
-        alpha[:, q * 128:(q + 1) * 128] = raw[:, q * 128:(q + 1) * 128] * scale
-    pltpu.make_async_copy(part.at[pl.ds(0, 7)], part.at[pl.ds(0, 7)], send).wait()
-
-
-def run_first(number, raw):
-    vmem = pl.BlockSpec(memory_space=pltpu.VMEM)
-    return pl.pallas_call(
-        first_kernel,
-        out_shape=(jax.ShapeDtypeStruct((SEQS, OWN), F32), jax.ShapeDtypeStruct((1, SEQS), F32)),
-        in_specs=[vmem],
-        out_specs=(vmem, vmem),
-        scratch_shapes=[
-            pltpu.VMEM((N_DEV, 1, 128), F32),
-            pltpu.VMEM((128, 128), F32),
-            pltpu.SemaphoreType.DMA,
-            pltpu.SemaphoreType.DMA,
-        ],
-        compiler_params=pltpu.CompilerParams(collective_id=number, has_side_effects=True, vmem_limit_bytes=8 << 20),
-        name="first",
-    )(raw)
-
-
-def step_kernel(m, steps, depth, t0_ref, a_hbm, e_hbm, st_in, len_row, ll_in, st_out, ll_out,
+def step_kernel(m, steps, depth, first, t0_ref, a_hbm, e_hbm, st_in, len_row, ll_in, st_out, ll_out,
                 fixed, ring, gath, e_buf, st, acc, part, sums, recip, len_col,
                 fixed_sem, ring_sem, e_sem, st_sem, recv_sem, own_sem, fwd_sem, c_send, c_recv):
     me = lax.axis_index("states")
@@ -206,9 +171,21 @@
     def total_sent(slot):
         pltpu.make_async_copy(part.at[slot, pl.ds(0, 7)], part.at[slot, pl.ds(0, 7)], c_send.at[slot]).wait()
 
-    ll_out[...] = ll_in[...]
     st_copy.wait()
-    pl.semaphore_wait(barrier, N_DEV - 1)
+    if first:
+        both = st[:, :128]
+        for q in range(1, 16):
+            both = both + st[:, q * 128:(q + 1) * 128]
+        sums[...] = both
+        pl.semaphore_wait(barrier, N_DEV - 1)
+        total(1)
+        ll_out[...] = jnp.log(total_done(1))
+        total_sent(1)
+        for q in range(16):
+            st[:, q * 128:(q + 1) * 128] = st[:, q * 128:(q + 1) * 128] * recip[...]
+    else:
+        ll_out[...] = ll_in[...]
+        pl.semaphore_wait(barrier, N_DEV - 1)
     for j in range(2):
         for i in (j, j + 2):
             gath[0, i] = st[:, i * PIECE:(i + 1) * PIECE].astype(BF16)
@@ -326,43 +303,44 @@
     out_copy.wait()
 
 
-def pick_kernel(size, ahead, rows, mods, emit, out, blocks, sem):
+def pick_kernel(size, ahead, tokens, odd, emit, out, blocks, sem):
     i = pl.program_id(0)
     slots = ahead + 1
 
-    def start(g):
-        for q in range(size):
-            row = pl.multiple_of(rows[g * size + q], 2)
-            pltpu.make_async_copy(
-                emit.at[pl.ds(row, 2)], blocks.at[g % slots, pl.ds(2 * q, 2)], sem.at[g % slots]
-            ).start()
+    def start(g, carry):
+        def some(c, carry):
+            for k in range(16):
+                q = 16 * c + k
+                row = pl.multiple_of((tokens[g * size + q] // 2) * 2, 2)
+                pltpu.make_async_copy(
+                    emit.at[pl.ds(row, 2)], blocks.at[g % slots, pl.ds(pl.multiple_of(2 * q, 2), 2)], sem.at[g % slots]
+                ).start()
+            return carry
+
+        return lax.fori_loop(0, size // 16, some, carry)
 
     @pl.when(i == 0)
     def _():
-        def some(g, carry):
-            start(g)
-            return carry
-
-        lax.fori_loop(0, ahead, some, 0)
+        lax.fori_loop(0, ahead, start, 0)
 
     @pl.when(i + ahead < pl.num_programs(0))
     def _():
-        start(i + ahead)
+        start(i + ahead, 0)
 
     slot = i % slots
     pltpu.make_async_copy(blocks.at[slot], blocks.at[slot], sem.at[slot]).wait()
     row = lax.broadcasted_iota(jnp.int32, (size, 2 * size), 0)
     col = lax.broadcasted_iota(jnp.int32, (size, 2 * size), 1)
-    want = row * 2 + mods[:, :2 * size]
+    want = row * 2 + jnp.concatenate([odd[...]] * 3, axis=1)[:, :2 * size]
     ones = (col == want).astype(F32).astype(BF16)
     out[...] = jnp.dot(ones, blocks[slot], preferred_element_type=F32).astype(BF16)
 
 
 def pick_rows(emit, tokens):
     (count,) = tokens.shape
-    size = 48 if count % 48 == 0 else 64
-    ahead = min(3, count // size)
-    mods = jnp.broadcast_to((tokens % 2)[:, None], (count, 128))
+    size = 144 if count % 144 == 0 else 64
+    ahead = min(2, count // size)
+    odd = jnp.broadcast_to((tokens & 1)[:, None], (count, 128))
     return pl.pallas_call(
         functools.partial(pick_kernel, size, ahead),
         out_shape=jax.ShapeDtypeStruct((count, OWN), BF16),
@@ -375,16 +353,16 @@
         ),
         compiler_params=pltpu.CompilerParams(vmem_limit_bytes=60 << 20),
         name="pick",
-    )(tokens - tokens % 2, mods, emit)
-
-
-def run_steps(m, steps, number, t0, trans, emis, state, len_row, log_lik):
+    )(tokens, odd, emit)
+
+
+def run_steps(m, steps, first, number, t0, trans, emis, state, len_row, log_lik):
     vmem = pl.BlockSpec(memory_space=pltpu.VMEM)
     hbm = pl.BlockSpec(memory_space=pl.ANY)
     depth = 2 if m > 80 else 4
     dma = pltpu.SemaphoreType.DMA
     return pl.pallas_call(
-        functools.partial(step_kernel, m, steps, depth),
+        functools.partial(step_kernel, m, steps, depth, first),
         out_shape=(jax.ShapeDtypeStruct((SEQS, OWN), F32), jax.ShapeDtypeStruct((1, SEQS), F32)),
         in_specs=[pl.BlockSpec(memory_space=pltpu.SMEM), hbm, hbm, hbm, vmem, vmem],
         out_specs=(hbm, vmem),
@@ -405,7 +383,7 @@
         compiler_params=pltpu.CompilerParams(
             collective_id=number, has_side_effects=True, vmem_limit_bytes=67043328
         ),
-        name=f"steps_{m}_{number}",
+        name=f"steps_{m}_{steps}_{number}",
     )(t0, trans, emis, state, len_row, log_lik)
 
 
@@ -423,23 +401,29 @@
         tokens = jnp.sum(token_rows.T[:, None, :] * pick[None], axis=2)
         len_row = lens[None, :]
 
-        def segment(m, number, t0, state, log_lik):
-            part = lax.dynamic_slice_in_dim(tokens, t0, SEGMENT, axis=0)[:, :m]
-            return run_steps(m, SEGMENT, number, jnp.reshape(t0, (1,)), trans_cols, emissions(part), state,
+        def segment(steps, first, m, number, t0, state, log_lik):
+            part = lax.dynamic_slice_in_dim(tokens, t0, steps, axis=0)[:, :m]
+            return run_steps(m, steps, first, number, jnp.reshape(t0, (1,)), trans_cols, emissions(part), state,
                              len_row, log_lik)
 
-        state, log_lik = run_first(0, init_part[None, :] * emissions(tokens[0]).astype(F32))
-
-        segs = jnp.arange(STEPS // SEGMENT, dtype=jnp.int32)
-        live = jnp.sum((lens[None, :] > 1 + SEGMENT * segs[:, None]).astype(jnp.int32), axis=1)
+        state = init_part[None, :] * emissions(tokens[0]).astype(F32)
+        state, log_lik = segment(SHORT, True, SEQS, 0, jnp.int32(1), state, jnp.zeros((1, SEQS), F32))
+
+        segs = jnp.arange(1, SEGMENTS, dtype=jnp.int32)
+        live = jnp.sum((lens[None, :] > 1 + SHORT * segs[:, None]).astype(jnp.int32), axis=1)
         which = sum((live > m).astype(jnp.int32) for m in ROWS[:-1])
+        which = jnp.where((segs == SEGMENTS - LONG) & (live <= LONG_ROWS), len(ROWS), which)
         plan = jnp.sum(which << (3 * segs))
 
-        def later(seg, carried):
-            branches = [functools.partial(segment, m, 1 + i) for i, m in enumerate(ROWS)]
-            return lax.switch((plan >> (3 * seg)) & 7, branches, 1 + SEGMENT * seg, *carried)
-
-        state, log_lik = lax.fori_loop(0, STEPS // SEGMENT, later, (state, log_lik))
+        def later(carried):
+            seg, state, log_lik = carried
+            kernel = (plan >> (3 * seg)) & 7
+            branches = [functools.partial(segment, SHORT, False, m, 1 + i) for i, m in enumerate(ROWS)]
+            branches.append(functools.partial(segment, SHORT * LONG, False, LONG_ROWS, 1 + len(ROWS)))
+            state, log_lik = lax.switch(kernel, branches, 1 + SHORT * seg, state, log_lik)
+            return seg + jnp.where(kernel == len(ROWS), LONG, 1), state, log_lik
+
+        _, state, log_lik = lax.while_loop(lambda carried: carried[0] < SEGMENTS, later, (jnp.int32(1), state, log_lik))
         return jnp.take(log_lik[0], rank, mode="clip"), jnp.take(state, rank, axis=0, mode="clip")
 
     return jax.shard_map(

time: 1370 us -> 1360 us (level)
    pallas_call x8 -> x6, Pallas kernels: 84.9 us -> 107 us  [pick_rows(): pl.pallas_call(functools.partial(pick_kernel, size, ahead), out_shape=jax...]
    pallas_call x8 -> x5, Pallas kernels: 1240 us -> 1220 us  [run_steps(): pl.pallas_call(functools.partial(step_kernel, m, steps, depth, first), ou...]
where the time goes in v2:
time: 1360 us
  Pallas kernels  1330 us (98%)
  local copies, waits for them, and re-layouts  16.4 us (1%)
    pallas_call x5, Pallas kernels, run_steps(): pl.pallas_call(functools.partial(step_kernel, m, steps, depth, first), ou...  1220 us
    pallas_call x6, Pallas kernels, pick_rows(): pl.pallas_call(functools.partial(pick_kernel, size, ahead), out_shape=jax...  107 us

profile of v2, /device:TPU:0, one launch (start us, length us, event | category | flops | bytes accessed | tf_op | source)
XLA Modules:
  0.0 1355.1 jit_solution(3673626436432343045)
XLA Ops:
  1.5 1.9 multiply_reduce_fusion
  4.0 1.0 broadcast_in_dim.32.odd
  5.1 21.3 %pick.14 = bf16[1152,2048]{1,0:T(8,128)(2,1)} custom-call(s32[1152]{0:T(1024)} %slice_bitcast_fusion.tokens, s32[1152,128]{1,0:T(8,128)} %broadcast_in_dim.32.odd, bf16[10000,2048]{1,0:T(8,128)(2,1)} %bitcast.28), custom_call_target="tpu_custom_call" | custom-call | tf_op jit(solution)/shard_map/pick/pallas_call | solution.py:344
  27.6 4.7 pick.15
  32.4 2.1 convert_multiply_fusion.st_in
  35.7 224.2 %steps_128_9_0.1 = (f32[128,2048]{1,0:T(8,128)}, f32[1,128]{1,0:T(1,128)}) custom-call(s32[1]{0:T(128)} %constant.13.clone.1.t0_ref, bf16[16384,2048]{1,0:T(8,128)(2,1)} %a_hbm.1, bf16[9,128,2048]{2,1,0:T(8,128)(2,1)} %bitcast.38, f32[128,2048]{1,0:T(8,128)} %convert_multiply_fusion.st_in, ...), custom_call_target="tpu_custom_call", output_to_operand_aliasing={{0}: (3, {}), {1}: (5, {})} | custom-call | tf_op jit(solution)/shard_map/steps_128_9_0/pallas_call | solution.py:364
  261.3 1087.5 %while.12 = (s32[]{:T(128)}, f32[128,2048]{1,0:T(8,128)}, f32[1,128]{1,0:T(1,128)}, s32[]{:T(128)}, s32[64,128]{1,0:T(8,128)}, /*index=5*/bf16[10000,2048]{1,0:T...) while((s32[]{:T(128)}, f32[128,2048]{1,0:T(8,128)}, ...), condition=%wide.region_12.13_spmd, body=%wide.region_5.12_spmd.sunk | while | flops 1741 | bytes 961137 | solution.py:426
  261.9 222.7 %conditional.2 = ((f32[128,2048]{1,0:T(8,128)}, f32[1,128]{1,0:T(1,128)})) conditional(s32[]{:T(128)} %clamp.7, (s32[]{:T(128)}, s32[64,128]{1,0:T(8,128)}, bf16[10000,2048]{1,0:T(8,128)(2,1)}, bf16[16384,2048]{1,0:T(8,128)(2,1)}, f32[128,2048]{1,0:T(8,128)}, /*index=5*/s32[1,128]{1,0:T(1,128)}, ...), branch_computations={%region_6.6_spmd, %region_7.7_spmd, %region_8.8_spmd, %region_9.9_... | conditional | flops 1731 | bytes 960842 | solution.py:423
  262.7 1.0 broadcast_in_dim.9.odd
  263.7 19.0 %pick.11 = bf16[1008,2048]{1,0:T(8,128)(2,1)} custom-call(s32[1008]{0:T(1024)} %copy-done.5, s32[1008,128]{1,0:T(8,128)} %broadcast_in_dim.9.odd, bf16[10000,2048]{1,0:T(8,128)(2,1)} %get-tuple-element.140.emit), custom_call_target="tpu_custom_call" | custom-call | tf_op jit(solution)/shard_map/while/body/cond/branch_3_fun/pick/pallas_call | solution.py:344
  282.7 201.8 %steps_112_9_4.1 = (f32[128,2048]{1,0:T(8,128)}, f32[1,128]{1,0:T(1,128)}) custom-call(s32[1]{0:T(128)} %bitcast.6.t0_ref, bf16[16384,2048]{1,0:T(8,128)(2,1)} %get-tuple-element.138.a_hbm, bf16[9,112,2048]{2,1,0:T(8,128)(2,1)} %bitcast.34, f32[128,2048]{1,0:T(8,128)} %get-tuple-element.141.st_in, ...), custom_call_target="tpu_custom_call", output_to_operand_aliasing={{0}: (3, {}), {1}: (5, {})} | custom-call | tf_op jit(solution)/shard_map/while/body/cond/branch_3_fun/steps_112_9_4/pallas_call | solution.py:364
  485.2 204.8 %conditional.2 = ((f32[128,2048]{1,0:T(8,128)}, f32[1,128]{1,0:T(1,128)})) conditional(s32[]{:T(128)} %clamp.7, (s32[]{:T(128)}, s32[64,128]{1,0:T(8,128)}, bf16[10000,2048]{1,0:T(8,128)(2,1)}, bf16[16384,2048]{1,0:T(8,128)(2,1)}, f32[128,2048]{1,0:T(8,128)}, /*index=5*/s32[1,128]{1,0:T(1,128)}, ...), branch_computations={%region_6.6_spmd, %region_7.7_spmd, %region_8.8_spmd, %region_9.9_... | conditional | flops 1731 | bytes 960842 | solution.py:423
  486.0 0.9 broadcast_in_dim.7.odd
  487.0 16.6 %pick.10 = bf16[864,2048]{1,0:T(8,128)(2,1)} custom-call(s32[864]{0:T(1024)} %copy-done.4, s32[864,128]{1,0:T(8,128)} %broadcast_in_dim.7.odd, bf16[10000,2048]{1,0:T(8,128)(2,1)} %get-tuple-element.133.emit), custom_call_target="tpu_custom_call" | custom-call | tf_op jit(solution)/shard_map/while/body/cond/branch_2_fun/pick/pallas_call | solution.py:344
  503.6 186.3 %steps_96_9_3.1 = (f32[128,2048]{1,0:T(8,128)}, f32[1,128]{1,0:T(1,128)}) custom-call(s32[1]{0:T(128)} %bitcast.4.t0_ref, bf16[16384,2048]{1,0:T(8,128)(2,1)} %get-tuple-element.131.a_hbm, bf16[9,96,2048]{2,1,0:T(8,128)(2,1)} %bitcast.35, f32[128,2048]{1,0:T(8,128)} %get-tuple-element.134.st_in, ...), custom_call_target="tpu_custom_call", output_to_operand_aliasing={{0}: (3, {}), {1}: (5, {})} | custom-call | tf_op jit(solution)/shard_map/while/body/cond/branch_2_fun/steps_96_9_3/pallas_call | solution.py:364
  690.6 186.0 %conditional.2 = ((f32[128,2048]{1,0:T(8,128)}, f32[1,128]{1,0:T(1,128)})) conditional(s32[]{:T(128)} %clamp.7, (s32[]{:T(128)}, s32[64,128]{1,0:T(8,128)}, bf16[10000,2048]{1,0:T(8,128)(2,1)}, bf16[16384,2048]{1,0:T(8,128)(2,1)}, f32[128,2048]{1,0:T(8,128)}, /*index=5*/s32[1,128]{1,0:T(1,128)}, ...), branch_computations={%region_6.6_spmd, %region_7.7_spmd, %region_8.8_spmd, %region_9.9_... | conditional | flops 1731 | bytes 960842 | solution.py:423
  692.3 14.3 %pick.9 = bf16[720,2048]{1,0:T(8,128)(2,1)} custom-call(s32[720]{0:T(1024)} %copy-done.3, s32[720,128]{1,0:T(8,128)} %broadcast_in_dim.5.odd, bf16[10000,2048]{1,0:T(8,128)(2,1)} %get-tuple-element.126.emit), custom_call_target="tpu_custom_call" | custom-call | tf_op jit(solution)/shard_map/while/body/cond/branch_1_fun/pick/pallas_call | solution.py:344
  706.6 169.9 %steps_80_9_2.1 = (f32[128,2048]{1,0:T(8,128)}, f32[1,128]{1,0:T(1,128)}) custom-call(s32[1]{0:T(128)} %bitcast.2.t0_ref, bf16[16384,2048]{1,0:T(8,128)(2,1)} %get-tuple-element.124.a_hbm, bf16[9,80,2048]{2,1,0:T(8,128)(2,1)} %bitcast.36, f32[128,2048]{1,0:T(8,128)} %get-tuple-element.127.st_in, ...), custom_call_target="tpu_custom_call", output_to_operand_aliasing={{0}: (3, {}), {1}: (5, {})} | custom-call | tf_op jit(solution)/shard_map/while/body/cond/branch_1_fun/steps_80_9_2/pallas_call | solution.py:364
  877.1 471.7 %conditional.2 = ((f32[128,2048]{1,0:T(8,128)}, f32[1,128]{1,0:T(1,128)})) conditional(s32[]{:T(128)} %clamp.7, (s32[]{:T(128)}, s32[64,128]{1,0:T(8,128)}, bf16[10000,2048]{1,0:T(8,128)(2,1)}, bf16[16384,2048]{1,0:T(8,128)(2,1)}, f32[128,2048]{1,0:T(8,128)}, /*index=5*/s32[1,128]{1,0:T(1,128)}, ...), branch_computations={%region_6.6_spmd, %region_7.7_spmd, %region_8.8_spmd, %region_9.9_... | conditional | flops 1731 | bytes 960842 | solution.py:423
  878.0 1.2 broadcast_in_dim.13.odd
  879.2 30.7 %pick.13 = bf16[1728,2048]{1,0:T(8,128)(2,1)} custom-call(s32[1728]{0:T(1024)} %copy-done.1, s32[1728,128]{1,0:T(8,128)} %broadcast_in_dim.13.odd, bf16[10000,2048]{1,0:T(8,128)(2,1)} %get-tuple-element.154.emit), custom_call_target="tpu_custom_call" | custom-call | tf_op jit(solution)/shard_map/while/body/cond/branch_5_fun/pick/pallas_call | solution.py:344
  909.9 438.8 %steps_64_27_6.1 = (f32[128,2048]{1,0:T(8,128)}, f32[1,128]{1,0:T(1,128)}) custom-call(s32[1]{0:T(128)} %bitcast.11.t0_ref, bf16[16384,2048]{1,0:T(8,128)(2,1)} %get-tuple-element.152.a_hbm, bf16[27,64,2048]{2,1,0:T(8,128)(2,1)} %bitcast.31, f32[128,2048]{1,0:T(8,128)} %get-tuple-element.155.st_in, ...), custom_call_target="tpu_custom_call", output_to_operand_aliasing={{0}: (3, {}), {1}: (5, {})} | custom-call | tf_op jit(solution)/shard_map/while/body/cond/branch_5_fun/steps_64_27_6/pallas_call | solution.py:364
  1349.4 2.1 gather_fusion
  1351.5 3.6 gather_fusion.1
  (43 shorter events, 10.0 us)
Async XLA Ops:
  1.5 33.0 %copy-start.7 = (s32[128]{0:T(128)}, s32[128]{0:T(128)S(1)}, u32[]{:S(2)}) copy-start(s32[128]{0:T(128)S(1)} %convert_reduce_fusion) | copy-start | bytes 1540
  3.4 23.5 %copy-start = (s32[64,128]{1,0:T(8,128)}, s32[64,128]{1,0:T(8,128)S(1)}, u32[]{:S(2)}) copy-start(s32[64,128]{1,0:T(8,128)S(1)} %multiply_reduce_fusion) | copy-start | bytes 98308
  27.6 4.7 copy-start.6
  27.6 6.9 copy-start.8
  262.7 1.0 copy-start.5
  486.0 1.0 copy-start.4
  691.4 0.9 copy-start.3
  878.0 1.2 copy-start.1
